TPU v7x, 32 devices: a whole 2x2x4 slice. The times are simulated.
32 devices in a mesh: rows: 8 (over z, y), cols: 4 (over x, core).
Axes of the slice: x: 2, y: 2, z: 4, core: 2. Of those that a mesh axis runs over, the one named last changes fastest.
Arguments:
- gradient: float32 [8192, 29568], P('rows', 'cols'), as said below
- start_block: float32 [29568, 64], P('cols'), may hold values from -0.03125 to 0.03125
- activations: float32 [512, 29568], P('rows', 'cols'), may hold values from -6 to 6
- out_grads: float32 [512, 8192], P('rows', 'cols'), may hold values from -6 to 6
Outputs:
- left_factor: float32 [8192, 64], P('rows')
- right_factor: float32 [29568, 64], P('cols')
- scores: float32 [512], P('rows')
Inputs may be any that keep to these rules, and one draw needn't show every extreme that they name: real-valued gradient entries, of order 29568 ** -0.5.
All inputs are finite; a program needn't handle non-finite values.
Results may differ from a plain program's by a relative error of at most 0.00013.
Values sent between devices are 32-bit elements; how exact they have to be, the bound alone decides.
A program may use at most 128 MiB of HBM per device.

v0:
```python
import jax
import jax.numpy as jnp
from jax import lax
from jax.sharding import PartitionSpec as P

ITERS = 2
HIGH = lax.Precision.HIGHEST


def factor_with(block, gram):
    lower = jnp.linalg.cholesky(gram)
    return (
        lax.linalg.triangular_solve(lower, block, left_side=False, lower=True, transpose_a=True),
        lower,
    )


def inner_gram(block):
    return jnp.dot(block.T, block, precision=HIGH, preferred_element_type=jnp.float32)


def per_device(gradient, start_block, activations, out_grads):
    grad_cols = out_grads.shape[1]
    col_index = lax.axis_index("cols")
    omega = start_block
    for step in range(ITERS):
        ysum = lax.psum(
            jnp.dot(gradient, omega, precision=HIGH, preferred_element_type=jnp.float32), "cols"
        )
        gram = lax.psum(inner_gram(ysum), "rows")
        left, lower_y = factor_with(ysum, gram)
        partial_z = jnp.dot(gradient.T, left, precision=HIGH, preferred_element_type=jnp.float32)
        zsum = lax.psum(partial_z, "rows")
        zgram = lax.psum(inner_gram(zsum), "cols")
        right, lower_z = factor_with(zsum, zgram)
        omega = right
    whole_rows = lax.all_gather(left, "rows", axis=0, tiled=True)
    left_cols = lax.dynamic_slice_in_dim(whole_rows, col_index * grad_cols, grad_cols, 0)
    left_part = jnp.dot(out_grads, left_cols, precision=HIGH, preferred_element_type=jnp.float32)
    right_part = jnp.dot(activations, right, precision=HIGH, preferred_element_type=jnp.float32)
    token_left, token_right = lax.psum((left_part, right_part), "cols")
    mixed = jnp.dot(token_left, lower_z, precision=HIGH, preferred_element_type=jnp.float32)
    scores = jnp.sum(mixed * token_right, axis=1)
    return (left, right, scores)


def solution(mesh):
    placed = (P("rows", "cols"), P("cols", None), P("rows", "cols"), P("rows", "cols"))
    return jax.shard_map(
        per_device,
        mesh=mesh,
        in_specs=placed,
        out_specs=(P("rows", None), P("cols", None), P("rows")),
        check_vma=False,
    )
```

profile of v0, /device:TPU:0, one launch (start us, length us, event | category | flops | bytes accessed | tf_op | source)
XLA Modules:
  0.0 579.3 jit_solution(6776016720726716855)
XLA Ops:
  7.2 1.5 copy-done
  8.7 24.2 %fusion.23 = f32[1024,64]{0,1:T(8,128)} fusion(f32[1024,7392]{0,1:T(8,128)} %param.9, f32[7392,64]{0,1:T(8,128)S(1)} %copy-done), kind=kOutput, calls=%fused_computation.50 | convolution fusion | flops 5813305344 | bytes 32432128 | tf_op jit(solution)/shard_map/dot_general | solution.py:28
  33.0 35.1 %all-reduce.6.cloned.1.call-done = f32[1024,64]{0,1:T(8,128)} async-done(((f32[1024,64]{0,1:T(8,128)}), f32[1024,64]{0,1:T(8,128)}) %all-reduce.6.cloned.1.call-update) | async-done | bytes 262160 | tf_op jit(solution)/shard_map/psum | solution.py:27
  68.1 1.4 fusion.24
  69.5 37.5 %psum.71 = f32[64,64]{0,1:T(8,128)S(1)} all-reduce(f32[64,64]{0,1:T(8,128)S(1)} %fusion.24), channel_id=1, replica_groups=mesh['rows'=8,'cols'=4] {'rows'}, use_global_device_ids=true, to_apply=%region_1.0 | all-reduce | flops 4096 | bytes 32768 | tf_op jit(solution)/shard_map/psum | solution.py:30
  107.1 5.8 %cholesky.74 = f32[64,64]{1,0:T(8,128)S(1)} custom-call(f32[64,64]{1,0:T(8,128)S(1)} %fusion.12), custom_call_target="Cholesky" | custom-call | tf_op jit(solution)/shard_map/jit(cholesky)/cholesky | solution.py:11
  114.3 4.9 custom-call.10
  120.6 30.9 %convolution_bitcast_fusion.3 = f32[7392,64]{0,1:T(8,128)} fusion(f32[1024,64]{0,1:T(8,128)S(1)} %convolution_bitcast_fusion.5, f32[1024,7392]{0,1:T(8,128)} %param.9), kind=kOutput, calls=%fused_computation.3 | convolution fusion | flops 5813305344 | bytes 32432128 | tf_op jit(solution)/shard_map/dot_general | solution.py:32
  151.5 93.6 %all-reduce.8.cloned.1.call-done = f32[7392,64]{0,1:T(8,128)} async-done(((f32[7392,64]{0,1:T(8,128)}), f32[7392,64]{0,1:T(8,128)}) %all-reduce.8.cloned.1.call-update) | async-done | bytes 1892368 | tf_op jit(solution)/shard_map/psum | solution.py:33
  245.1 3.8 fusion.25
  248.9 11.9 %psum.73 = f32[64,64]{0,1:T(8,128)S(1)} all-reduce(f32[64,64]{0,1:T(8,128)S(1)} %fusion.25), channel_id=1, replica_groups=mesh['rows'=8,'cols'=4] {'cols'}, use_global_device_ids=true, to_apply=%region_5.8 | all-reduce | flops 4096 | bytes 32768 | tf_op jit(solution)/shard_map/psum | solution.py:34
  260.9 5.8 %cholesky.85 = f32[64,64]{1,0:T(8,128)S(1)} custom-call(f32[64,64]{1,0:T(8,128)S(1)} %fusion.10), custom_call_target="Cholesky" | custom-call | tf_op jit(solution)/shard_map/jit(cholesky)/cholesky | solution.py:11
  268.1 4.9 custom-call.11
  273.0 3.3 convolution_bitcast_fusion.2
  276.2 23.1 %convolution_bitcast_fusion.6 = f32[1024,64]{0,1:T(8,128)} fusion(f32[7392,64]{0,1:T(8,128)S(1)} %convolution_bitcast_fusion.2, f32[1024,7392]{0,1:T(8,128)} %param.9), kind=kOutput, calls=%fused_computation.6 | convolution fusion | flops 5813305344 | bytes 32432128 | tf_op jit(solution)/shard_map/dot_general | solution.py:28
  299.4 31.0 %all-reduce.10.cloned.1.call-done = f32[1024,64]{0,1:T(8,128)} async-done(((f32[1024,64]{0,1:T(8,128)}), f32[1024,64]{0,1:T(8,128)}) %all-reduce.10.cloned.1.call-update) | async-done | bytes 262160 | tf_op jit(solution)/shard_map/psum | solution.py:27
  330.5 1.4 fusion.26
  331.9 37.4 %psum.75 = f32[64,64]{0,1:T(8,128)S(1)} all-reduce(f32[64,64]{0,1:T(8,128)S(1)} %fusion.26), channel_id=1, replica_groups=mesh['rows'=8,'cols'=4] {'rows'}, use_global_device_ids=true, to_apply=%region_7.11 | all-reduce | flops 4096 | bytes 32768 | tf_op jit(solution)/shard_map/psum | solution.py:30
  369.4 5.8 %cholesky.96 = f32[64,64]{1,0:T(8,128)S(1)} custom-call(f32[64,64]{1,0:T(8,128)S(1)} %fusion.8), custom_call_target="Cholesky" | custom-call | tf_op jit(solution)/shard_map/jit(cholesky)/cholesky | solution.py:11
  376.6 4.9 custom-call.12
  381.5 1.4 convolution_bitcast_fusion.4
  382.9 31.0 %convolution_bitcast_fusion.1 = f32[7392,64]{0,1:T(8,128)} fusion(f32[1024,64]{0,1:T(8,128)S(1)} %convolution_bitcast_fusion.4, f32[1024,7392]{0,1:T(8,128)} %param.9), kind=kOutput, calls=%fused_computation.1 | convolution fusion | flops 5813305344 | bytes 32432128 | tf_op jit(solution)/shard_map/dot_general | solution.py:32
  414.5 93.0 %all-reduce.12.cloned.1.call-done = f32[7392,64]{0,1:T(8,128)} async-done(((f32[7392,64]{0,1:T(8,128)}), f32[7392,64]{0,1:T(8,128)}) %all-reduce.12.cloned.1.call-update) | async-done | bytes 1892368 | tf_op jit(solution)/shard_map/psum | solution.py:33
  507.4 3.8 fusion.27
  511.2 11.6 %psum.77 = f32[64,64]{0,1:T(8,128)S(1)} all-reduce(f32[64,64]{0,1:T(8,128)S(1)} %fusion.27), channel_id=1, replica_groups=mesh['rows'=8,'cols'=4] {'cols'}, use_global_device_ids=true, to_apply=%region_9.13 | all-reduce | flops 4096 | bytes 32768 | tf_op jit(solution)/shard_map/psum | solution.py:34
  522.9 5.8 %cholesky.107 = f32[64,64]{1,0:T(8,128)S(1)} custom-call(f32[64,64]{1,0:T(8,128)S(1)} %fusion.6), custom_call_target="Cholesky" | custom-call | tf_op jit(solution)/shard_map/jit(cholesky)/cholesky | solution.py:11
  530.0 4.9 custom-call.13
  534.9 3.4 convolution_bitcast_fusion
  539.6 1.7 convolution_bitcast_fusion.7
  541.3 17.6 %all-gather.2.cloned.1.call-done = f32[8192,64]{0,1:T(8,128)} async-done(((f32[1024,64]{0,1:T(8,128)}), f32[8192,64]{0,1:T(8,128)}) %all-gather.2.cloned.1.call-update) | async-done | bytes 2097168 | tf_op jit(solution)/shard_map/all_gather | solution.py:37
  558.9 1.6 convolution_bitcast_fusion.8
  560.5 10.7 %all-reduce = (f32[64,64]{0,1:T(8,128)S(1)}, f32[64,64]{0,1:T(8,128)S(1)}) all-reduce(f32[64,64]{0,1:T(8,128)S(1)} %convolution_bitcast_fusion.7, f32[64,64]{0,1:T(8,128)S(1)} %convolution_bitcast_fusion.8), channel_id=1, replica_groups=mesh['rows'=8,'cols'=4] {'cols'}, use_global_device_ids=true, to_apply=%region_11.15 | all-reduce | flops 8192 | bytes 65536 | tf_op jit(solution)/shard_map/psum | solution.py:41
  (41 shorter events, 10.3 us)
Async XLA Ops:
  7.2 1.5 copy-start
  7.2 60.9 %all-reduce.6.cloned.1.call-start = ((), (), s32[]{:S(2)}) async-start(), calls=%async_computation | async-start | bytes 524288 | tf_op jit(solution)/shard_map/psum | solution.py:27
  32.9 212.2 %all-reduce.8.cloned.1.call-start = ((), (), s32[]{:S(2)}) async-start(), calls=%async_computation.1 | async-start | bytes 3801088 | tf_op jit(solution)/shard_map/psum | solution.py:33
  151.5 179.0 %all-reduce.10.cloned.1.call-start = ((), (), s32[]{:S(2)}) async-start(), calls=%async_computation.2 | async-start | bytes 524288 | tf_op jit(solution)/shard_map/psum | solution.py:27
  299.4 208.0 %all-reduce.12.cloned.1.call-start = ((), (), s32[]{:S(2)}) async-start(), calls=%async_computation.3 | async-start | bytes 3801088 | tf_op jit(solution)/shard_map/psum | solution.py:33
  382.8 31.0 %copy-start.2 = (f32[1024,64]{0,1:T(8,128)}, f32[1024,64]{0,1:T(8,128)S(1)}, u32[]{:S(2)}) copy-start(f32[1024,64]{0,1:T(8,128)S(1)} %convolution_bitcast_fusion.4) | copy-start | bytes 786436
  413.9 145.0 %all-gather.2.cloned.1.call-start = ((), (), s32[]{:S(2)}) async-start(), calls=%async_computation.4 | async-start | bytes 2359296 | tf_op jit(solution)/shard_map/all_gather | solution.py:37
  534.9 4.7 copy-start.3
  538.3 1.3 copy-start.1
  539.6 19.3 %copy-start.4 = (f32[64,2048]{1,0:T(8,128)S(1)}, f32[64,2048]{1,0:T(8,128)}, u32[]{:S(2)}) copy-start(f32[64,2048]{1,0:T(8,128)} %param.12) | copy-start | bytes 1572868
Sparse Core Ops, SparseCore 0:
  33.0 35.0 all-reduce.5
  151.6 93.4 all-reduce.7
  299.5 30.9 all-reduce.9
  414.0 93.4 all-reduce.11
  510.1 48.7 all-gather.1
where the time goes:
time: 583 us; the launch traced here: 579 us
  waiting for transfers between devices  271 us (46%)
  matrix products  133 us (23%)
  blocking collectives  109 us (19%)
  other arithmetic  48.2 us (8%)
  between operations  14.2 us (2%)
    psum x2, waiting for transfers between devices, per_device(): zsum = lax.psum(partial_z, 'rows')  187 us
    psum x2, blocking collectives, per_device(): gram = lax.psum(inner_gram(ysum), 'rows')  74.9 us
    psum x2, waiting for transfers between devices, per_device(): lax.psum(jnp.dot(gradient, omega, precision=HIGH, preferred_element_type=...  66.2 us
    dot_general x2, matrix products, per_device(): jnp.dot(gradient.T, left, precision=HIGH, preferred_element_type=jnp.floa...  61.9 us
    dot_general x2, matrix products, per_device(): jnp.dot(gradient, omega, precision=HIGH, preferred_element_type=jnp.float32)  47.3 us
    another operation x12, other arithmetic, factor_with(): lower = jnp.linalg.cholesky(gram)  26.1 us
    psum x2, blocking collectives, per_device(): zgram = lax.psum(inner_gram(zsum), 'cols')  23.5 us
    another operation x8, other arithmetic, factor_with(): lax.linalg.triangular_solve(lower, block, left_side=False, lower=True, tr...  22.1 us
  transfers between devices with their start and end apart: 5, of which 5 were waited for; matrix products, arithmetic and copies ran while one was open for 4% of the time, Pallas kernels for 0%

commit v1 on v0

--- a/solution.py
+++ b/solution.py
@@ -30,7 +30,7 @@
         gram = lax.psum(inner_gram(ysum), "rows")
         left, lower_y = factor_with(ysum, gram)
         partial_z = jnp.dot(gradient.T, left, precision=HIGH, preferred_element_type=jnp.float32)
-        zsum = lax.psum(partial_z, "rows")
+        zsum = jnp.sum(lax.all_gather(partial_z, "rows"), axis=0)
         zgram = lax.psum(inner_gram(zsum), "cols")
         right, lower_z = factor_with(zsum, zgram)
         omega = right

time: 583 us -> 811 us (1.39)
  waiting for transfers between devices: 271 us -> 488 us
  other arithmetic: 48.2 us -> 61 us
    all_gather x0 -> x2, waiting for transfers between devices: none -> 412 us  [per_device(): zsum = jnp.sum(lax.all_gather(partial_z, 'rows'), axis=0)]
    psum x2 -> x0, waiting for transfers between devices: 187 us -> none  [per_device(): zsum = lax.psum(partial_z, 'rows')]
    reduce_sum x0 -> x2, other arithmetic: none -> 12.6 us  [per_device(): zsum = jnp.sum(lax.all_gather(partial_z, 'rows'), axis=0)]
  transfers between devices with their start and end apart: 5 -> 5, of which waited for: 5 -> 5; matrix products, arithmetic and copies ran while one was open for 4% -> 5% of each run, Pallas kernels for 0% -> 0%
where the time goes in v1:
time: 811 us; the launch traced here: 807 us
  waiting for transfers between devices  488 us (60%)
  matrix products  133 us (16%)
  blocking collectives  107 us (13%)
  other arithmetic  61 us (8%)
  between operations  14.3 us (2%)
    all_gather x2, waiting for transfers between devices, per_device(): zsum = jnp.sum(lax.all_gather(partial_z, 'rows'), axis=0)  412 us
    psum x2, blocking collectives, per_device(): gram = lax.psum(inner_gram(ysum), 'rows')  74.6 us
    dot_general x2, matrix products, per_device(): jnp.dot(gradient.T, left, precision=HIGH, preferred_element_type=jnp.floa...  66.2 us
    psum x2, waiting for transfers between devices, per_device(): lax.psum(jnp.dot(gradient, omega, precision=HIGH, preferred_element_type=...  65.8 us
    dot_general x2, matrix products, per_device(): jnp.dot(gradient, omega, precision=HIGH, preferred_element_type=jnp.float32)  47.3 us
    another operation x12, other arithmetic, factor_with(): lower = jnp.linalg.cholesky(gram)  26.2 us
    another operation x8, other arithmetic, factor_with(): lax.linalg.triangular_solve(lower, block, left_side=False, lower=True, tr...  22.3 us
    psum x2, blocking collectives, per_device(): zgram = lax.psum(inner_gram(zsum), 'cols')  21.3 us
  transfers between devices with their start and end apart: 5, of which 5 were waited for; matrix products, arithmetic and copies ran while one was open for 5% of the time, Pallas kernels for 0%

profile of v1, /device:TPU:0, one launch (start us, length us, event | category | flops | bytes accessed | tf_op | source)
XLA Modules:
  0.0 806.7 jit_solution(7059181469929115836)
XLA Ops:
  7.2 1.5 copy-done
  8.7 24.2 %fusion.23 = f32[1024,64]{0,1:T(8,128)} fusion(f32[1024,7392]{0,1:T(8,128)} %param.9, f32[7392,64]{0,1:T(8,128)S(1)} %copy-done), kind=kOutput, calls=%fused_computation.50 | convolution fusion | flops 5813305344 | bytes 32432128 | tf_op jit(solution)/shard_map/dot_general | solution.py:28
  33.0 35.1 %all-reduce.4.cloned.1.call-done = f32[1024,64]{0,1:T(8,128)} async-done(((f32[1024,64]{0,1:T(8,128)}), f32[1024,64]{0,1:T(8,128)}) %all-reduce.4.cloned.1.call-update) | async-done | bytes 262160 | tf_op jit(solution)/shard_map/psum | solution.py:27
  69.5 37.5 %psum.57 = f32[64,64]{0,1:T(8,128)S(1)} all-reduce(f32[64,64]{0,1:T(8,128)S(1)} %fusion.24), channel_id=1, replica_groups=mesh['rows'=8,'cols'=4] {'rows'}, use_global_device_ids=true, to_apply=%region_1.0 | all-reduce | flops 4096 | bytes 32768 | tf_op jit(solution)/shard_map/psum | solution.py:30
  107.1 5.8 cholesky.74
  114.2 4.9 custom-call.10
  120.5 30.9 %convolution_bitcast_fusion.3 = f32[1,7392,64]{1,2,0:T(8,128)} fusion(f32[1024,64]{0,1:T(8,128)S(1)} %convolution_bitcast_fusion.5, f32[1024,7392]{0,1:T(8,128)} %param.9), kind=kOutput, calls=%fused_computation.3 | convolution fusion | flops 5813305344 | bytes 32432128 | tf_op jit(solution)/shard_map/dot_general | solution.py:32
  151.5 204.4 %all-gather.10.cloned.1.call-done = f32[8,7392,64]{1,2,0:T(8,128)} async-done(((f32[1,7392,64]{1,2,0:T(8,128)}), f32[8,7392,64]{1,2,0:T(8,128)}) %all-gather.10.cloned.1.call-update) | async-done | bytes 15138832 | tf_op jit(solution)/shard_map/all_gather | solution.py:33
  355.9 6.3 reduce_sum.27
  362.2 1.6 fusion.25
  363.8 10.9 %psum.58 = f32[64,64]{0,1:T(8,128)S(1)} all-reduce(f32[64,64]{0,1:T(8,128)S(1)} %fusion.25), channel_id=1, replica_groups=mesh['rows'=8,'cols'=4] {'cols'}, use_global_device_ids=true, to_apply=%region_5.8 | all-reduce | flops 4096 | bytes 32768 | tf_op jit(solution)/shard_map/psum | solution.py:34
  374.8 5.8 cholesky.85
  382.0 4.9 custom-call.11
  386.9 1.8 convolution_bitcast_fusion.2
  388.7 23.1 %convolution_bitcast_fusion.6 = f32[1024,64]{0,1:T(8,128)} fusion(f32[7392,64]{0,1:T(8,128)S(1)} %convolution_bitcast_fusion.2, f32[1024,7392]{0,1:T(8,128)} %param.9), kind=kOutput, calls=%fused_computation.6 | convolution fusion | flops 5813305344 | bytes 32432128 | tf_op jit(solution)/shard_map/dot_general | solution.py:28
  411.9 30.7 %all-reduce.6.cloned.1.call-done = f32[1024,64]{0,1:T(8,128)} async-done(((f32[1024,64]{0,1:T(8,128)}), f32[1024,64]{0,1:T(8,128)}) %all-reduce.6.cloned.1.call-update) | async-done | bytes 262160 | tf_op jit(solution)/shard_map/psum | solution.py:27
  444.0 37.1 %psum.60 = f32[64,64]{0,1:T(8,128)S(1)} all-reduce(f32[64,64]{0,1:T(8,128)S(1)} %fusion.26), channel_id=1, replica_groups=mesh['rows'=8,'cols'=4] {'rows'}, use_global_device_ids=true, to_apply=%region_7.11 | all-reduce | flops 4096 | bytes 32768 | tf_op jit(solution)/shard_map/psum | solution.py:30
  481.2 5.9 cholesky.96
  488.4 4.9 custom-call.12
  493.3 2.1 convolution_bitcast_fusion.4
  495.6 35.3 %convolution_bitcast_fusion.1 = f32[1,7392,64]{1,2,0:T(8,128)} fusion(f32[1024,64]{0,1:T(8,128)} %convolution_bitcast_fusion.4, f32[1024,7392]{0,1:T(8,128)} %param.9), kind=kOutput, calls=%fused_computation.1 | convolution fusion | flops 5813305344 | bytes 32432128 | tf_op jit(solution)/shard_map/dot_general | solution.py:32
  530.9 10.0 %all-gather.8.cloned.1.call-done = f32[8192,64]{0,1:T(8,128)} async-done(((f32[1024,64]{0,1:T(8,128)}), f32[8192,64]{0,1:T(8,128)}) %all-gather.8.cloned.1.call-update) | async-done | bytes 2097168 | tf_op jit(solution)/shard_map/all_gather | solution.py:37
  540.9 1.6 convolution_bitcast_fusion.8
  542.5 207.6 %all-gather.12.cloned.1.call-done = f32[8,7392,64]{1,2,0:T(8,128)} async-done(((f32[1,7392,64]{1,2,0:T(8,128)}), f32[8,7392,64]{1,2,0:T(8,128)}) %all-gather.12.cloned.1.call-update) | async-done | bytes 15138832 | tf_op jit(solution)/shard_map/all_gather | solution.py:33
  750.2 6.3 reduce_sum.28
  756.5 1.6 fusion.27
  758.1 10.3 %psum.61 = f32[64,64]{0,1:T(8,128)S(1)} all-reduce(f32[64,64]{0,1:T(8,128)S(1)} %fusion.27), channel_id=1, replica_groups=mesh['rows'=8,'cols'=4] {'cols'}, use_global_device_ids=true, to_apply=%region_9.13 | all-reduce | flops 4096 | bytes 32768 | tf_op jit(solution)/shard_map/psum | solution.py:34
  768.5 5.8 cholesky.107
  775.9 4.9 custom-call.13
  780.8 3.4 convolution_bitcast_fusion
  785.4 1.7 convolution_bitcast_fusion.7
  787.1 11.4 %all-reduce = (f32[64,64]{0,1:T(8,128)S(1)}, f32[64,64]{0,1:T(8,128)S(1)}) all-reduce(f32[64,64]{0,1:T(8,128)S(1)} %convolution_bitcast_fusion.7, f32[64,64]{0,1:T(8,128)S(1)} %convolution_bitcast_fusion.8), channel_id=1, replica_groups=mesh['rows'=8,'cols'=4] {'cols'}, use_global_device_ids=true, to_apply=%region_11.15 | all-reduce | flops 8192 | bytes 65536 | tf_op jit(solution)/shard_map/psum | solution.py:41
  (45 shorter events, 13.1 us)
Async XLA Ops:
  7.2 1.5 copy-start
  7.2 60.9 %all-reduce.4.cloned.1.call-start = ((), (), s32[]{:S(2)}) async-start(), calls=%async_computation | async-start | bytes 524288 | tf_op jit(solution)/shard_map/psum | solution.py:27
  32.9 323.0 %all-gather.10.cloned.1.call-start = ((), (), s32[]{:S(2)}) async-start(), calls=%async_computation.3 | async-start | bytes 17104896 | tf_op jit(solution)/shard_map/all_gather | solution.py:33
  151.4 291.1 %all-reduce.6.cloned.1.call-start = ((), (), s32[]{:S(2)}) async-start(), calls=%async_computation.1 | async-start | bytes 524288 | tf_op jit(solution)/shard_map/psum | solution.py:27
  411.9 129.0 %all-gather.8.cloned.1.call-start = ((), (), s32[]{:S(2)}) async-start(), calls=%async_computation.2 | async-start | bytes 2359296 | tf_op jit(solution)/shard_map/all_gather | solution.py:37
  495.4 254.8 %all-gather.12.cloned.1.call-start = ((), (), s32[]{:S(2)}) async-start(), calls=%async_computation.4 | async-start | bytes 17104896 | tf_op jit(solution)/shard_map/all_gather | solution.py:33
  530.9 10.0 %copy-start.5 = (f32[64,2048]{1,0:T(8,128)S(1)}, f32[64,2048]{1,0:T(8,128)}, u32[]{:S(2)}) copy-start(f32[64,2048]{1,0:T(8,128)} %param.12) | copy-start | bytes 1572868
  756.4 1.6 copy-start.2
  780.8 4.7 copy-start.4
  780.8 19.2 %copy-start.1 = (f32[7392,64]{0,1:T(8,128)S(1)}, f32[7392,64]{0,1:T(8,128)}, u32[]{:S(2)}) copy-start(f32[7392,64]{0,1:T(8,128)} %param.10) | copy-start | bytes 5677060
  784.2 1.3 copy-start.3
Sparse Core Ops, SparseCore 0:
  33.0 34.9 all-reduce.3
  151.6 204.2 all-gather.9
  412.0 30.5 all-reduce.5
  495.5 45.3 all-gather.7
  543.5 206.5 all-gather.11
